TPU v7x, 512 devices: a 4x2x32 block of a 4x8x32 slice. The times are simulated.
512 devices in a mesh: grp: 2 (over y), sp: 128 (over x, z), ch: 2 (over core).
Axes of the slice: x: 4, y: 2, z: 32, core: 2. Of those that a mesh axis runs over, the one named last changes fastest.
The devices are a block of a 4x8x32 slice.
Arguments:
- latents: bfloat16 [262144, 1024], P(('grp', 'sp')), parts along dimension 0, may hold values from -6 to 6
- spectrum: bfloat16 [16, 64, 128, 1024], P(None, None, 'sp', 'ch'), may hold values from -4 to 4
- w_value: bfloat16 [1024, 1024], P('sp', 'ch'), may hold values from -0.1875 to 0.1875
- w_gate: bfloat16 [1024, 1024], P('sp', 'ch'), may hold values from -0.1875 to 0.1875
- w_out: bfloat16 [1024, 1024], P('sp'), may hold values from -0.1875 to 0.1875
- embed_table: bfloat16 [1024, 32768], P(('sp', 'ch')), may hold values from -12 to 12
- prompt_ids: int32 [512], P('grp'), parts along dimension 0, may hold values from 0 to 32767
- noise_step: int32 [2], P('grp'), parts along dimension 0, may hold values from 0 to 999
Outputs:
- denoised: bfloat16 [262144, 1024], P(('grp', 'sp', 'ch')), parts along dimension 0
There are 2 independent parts, one for each index of `grp`. A program takes and returns all parts, laid end to end along the dimension named above; an argument that names none is the same for every part. Nothing has to cross between parts.
All inputs are finite; a program needn't handle non-finite values.
Results may differ from a plain program's by a relative error of at most 0.013.
Values may be sent and summed in bfloat16 or wider, within the bound.
A program may use at most 64 MiB of HBM per device.

v0:
```python
import math
import jax
import jax.numpy as jnp
from jax import lax
from jax.sharding import Mesh
from jax.sharding import PartitionSpec as P

TT = 16
HH = 64
WW = 128
C = 1024
SP = ("sp_0", "sp_1")
SP_CH = ("sp_0", "sp_1", "ch")
GRP_SP = ("grp", "sp_0", "sp_1")
GRP_SP_CH = ("grp", "sp_0", "sp_1", "ch")


def in_one_piece(arrays, axis, dim, along):
    ends, at = ([], 0)
    for a in arrays[:-1]:
        at += a.shape[along]
        ends.append(at)
    both = jnp.concatenate(arrays, axis=along)
    return tuple(jnp.split(lax.all_gather(both, axis, axis=dim, tiled=True), ends, axis=along))


def joined_along(parts, dim):
    lengths = list(parts.shape[1:])
    lengths[dim] *= parts.shape[0]
    return jnp.moveaxis(parts, 0, dim).reshape(lengths)


def gather_in_order(value, axes, sequence):
    parts = value[None]
    for k in sequence:
        parts = lax.all_gather(parts, axes[k], axis=0, tiled=True)
    held = [lax.axis_size(axes[k]) for k in reversed(sequence)]
    parts = parts.reshape(*held, *value.shape)
    turned = sorted(range(len(sequence)), key=lambda place: sequence[len(sequence) - 1 - place])
    return parts.transpose(*turned, *range(len(sequence), parts.ndim)).reshape(-1, *value.shape)


def gather_axes(value, axes, sequence, dim):
    return joined_along(gather_in_order(value, axes, sequence), dim)


def cas_table(length):
    position = jnp.arange(length, dtype=jnp.int32)
    product = position[:, None] * position[None, :] % length
    phase_angle = product.astype(jnp.float32) * (2.0 * math.pi / length)
    return ((jnp.cos(phase_angle) + jnp.sin(phase_angle)) / math.sqrt(length)).astype(jnp.bfloat16)


def step_embedding(noise_step, channel, channels):
    half_count = channels // 2
    lower_half = channel < half_count
    position = jnp.where(lower_half, channel, channel - half_count).astype(jnp.float32)
    frequency = jnp.exp(-math.log(10000.0) * position / half_count)
    phase_angle = noise_step[0].astype(jnp.float32) * frequency
    return jnp.where(lower_half, jnp.sin(phase_angle), jnp.cos(phase_angle))


def apply_table(form, table, operand):
    return jnp.einsum(form, table, operand, preferred_element_type=jnp.float32)


def local(latents, spectrum, w_value, w_gate, w_out, embed_table, prompt_ids, noise_step):
    row_count = latents.shape[0]
    chan_part = w_value.shape[1]
    full_value, full_gate, full_out = in_one_piece((w_value, w_gate, w_out), SP, 0, 1)
    value_rows = jnp.dot(latents, full_value, preferred_element_type=jnp.float32).astype(
        jnp.bfloat16
    )
    gate_rows = jnp.dot(latents, full_gate, preferred_element_type=jnp.float32)
    cas_width = cas_table(WW)
    cas_height = cas_table(HH)
    cas_time = cas_table(TT)
    line_grid = value_rows.reshape(row_count // WW, WW, chan_part)
    width_spec = apply_table("kw,lwc->lkc", cas_width, line_grid).astype(jnp.bfloat16)
    pencil = lax.all_to_all(width_spec, SP, split_axis=1, concat_axis=0, tiled=True)
    band_count = pencil.shape[1]
    pencil = pencil.reshape(TT, HH, band_count, chan_part)
    height_spec = apply_table("ah,thkc->takc", cas_height, pencil).astype(jnp.bfloat16)
    full_spec = apply_table("st,takc->sakc", cas_time, height_spec).astype(jnp.bfloat16)
    filtered = (full_spec.astype(jnp.float32) * spectrum.astype(jnp.float32)).astype(jnp.bfloat16)
    time_back = apply_table("ts,sakc->takc", cas_time, filtered).astype(jnp.bfloat16)
    height_back = apply_table("ha,takc->thkc", cas_height, time_back).astype(jnp.bfloat16)
    returned = lax.all_to_all(
        height_back.reshape(TT * HH, band_count, chan_part),
        SP,
        split_axis=0,
        concat_axis=1,
        tiled=True,
    )
    mix_rows = apply_table("wk,lkc->lwc", cas_width, returned).reshape(row_count, chan_part)
    offset = lax.axis_index("ch") * chan_part
    local_pool = jnp.mean(jnp.take(embed_table, prompt_ids, axis=1).astype(jnp.float32), axis=1)
    pooled_all = gather_axes(local_pool, SP_CH, (0, 1, 2), 0)
    pooled = lax.dynamic_slice_in_dim(pooled_all, offset, chan_part)
    channel = offset + jnp.arange(chan_part, dtype=jnp.int32)
    modulation = 1.0 + pooled + step_embedding(noise_step, channel, C)
    mixed_rows = (mix_rows * jax.nn.silu(gate_rows) * modulation[None, :]).astype(jnp.bfloat16)
    half_rows = row_count // lax.axis_size("ch")
    moved_rows = lax.all_to_all(mixed_rows, "ch", split_axis=0, concat_axis=1, tiled=True)
    summed = jnp.dot(moved_rows, full_out, preferred_element_type=jnp.float32)
    residual = lax.dynamic_slice_in_dim(latents, lax.axis_index("ch") * half_rows, half_rows, 0)
    return (residual.astype(jnp.float32) + summed).astype(jnp.bfloat16)


def solution(mesh):
    torus = Mesh(
        mesh.devices.reshape(mesh.shape["grp"], 4, 32, mesh.shape["ch"]),
        ("grp", "sp_0", "sp_1", "ch"),
    )
    in_specs = (
        P(GRP_SP, None),
        P(None, None, SP, "ch"),
        P(SP, "ch"),
        P(SP, "ch"),
        P(SP, None),
        P(SP_CH, None),
        P("grp"),
        P("grp"),
    )
    out_specs = P(GRP_SP_CH, None)
    return jax.shard_map(local, mesh=torus, in_specs=in_specs, out_specs=out_specs, check_vma=False)
```

profile of v0, /device:TPU:39, one launch (start us, length us, event | category | flops | bytes accessed | tf_op | source)
XLA Modules:
  0.0 582.0 jit_solution(15386378072836665653)
XLA Ops:
  6.5 0.0 all-gather.4.cloned.1.call-start
  6.6 1.3 pad_maximum_fusion
  7.9 0.1 all-gather.4.cloned.1.call-update
  8.0 275.0 %all-gather.4.cloned.1.call-done = bf16[1024,2048]{1,0:T(8,128)(2,1)} async-done(((bf16[8,2048]{1,0:T(8,128)(2,1)}), bf16[1024,2048]{1,0:T(8,128)(2,1)}) %all-gather.4.cloned.1.call-update) | async-done | bytes 4194320 | tf_op jit(solution)/shard_map/all_gather | solution.py:24
  282.9 3.2 fusion.11
  286.2 0.7 fusion.12
  286.9 0.9 copy.34
  287.8 0.0 copy-start
  287.8 104.4 %all_to_all.52 = bf16[8,128,512]{2,0,1:T(8,128)(2,1)S(1)} all-to-all(bf16[8,128,512]{2,0,1:T(8,128)(2,1)S(1)} %copy.34), channel_id=1, replica_groups=mesh['grp'=2,'sp_0'=4,'sp_1'=32,'ch'=2] {'sp_0','sp_1'}, dimensions={1} | all-to-all | bytes 2097152 | tf_op jit(solution)/shard_map/all_to_all | solution.py:80
  392.2 0.5 fusion.14
  392.8 0.0 copy-done
  392.8 1.6 convolution_convert_fusion.2
  394.4 1.5 convolution_convert_fusion
  395.9 0.5 broadcast.90
  396.4 1.5 reduce.1
  397.9 0.0 copy-start.1
  397.9 1.2 reshape.84
  399.1 16.2 %all-to-all-start.1 = ((bf16[128,2,2048]{2,1,0:T(2,128)(2,1)}), bf16[128,2,2048]{2,1,0:T(2,128)(2,1)S(1)}, u32[]{:S(2)}, u32[]{:S(2)}) async-start(bf16[128,2,2048]{2,1,0:T(2,128)(2,1)} %reshape.84), calls=%async_computation.1 | async-start | bytes 2097152 | tf_op jit(solution)/shard_map/all_to_all | solution.py:88
  415.3 0.0 copy-done.1
  415.3 0.0 copy-start.2
  415.3 5.7 copy.41
  421.1 1.3 dynamic-slice
  423.0 0.0 copy-done.2
  423.1 5.2 gather_fusion
  428.3 0.1 convert_reduce_fusion
  428.4 0.1 multiply_dynamic-update-slice_fusion
  428.5 6.2 %all-reduce = f32[16]{0:T(128)S(1)} all-reduce(f32[16]{0:T(128)S(1)} %multiply_dynamic-update-slice_fusion), channel_id=2, replica_groups=mesh['grp'=2,'sp_0'=4,'sp_1'=32,'ch'=2] {'sp_0'}, use_global_device_ids=true, to_apply=%add | all-reduce | flops 16 | bytes 128
  434.7 0.1 reshape.76
  434.8 97.6 %all-gather.1 = f32[32,4,4]{2,1,0:T(4,128)S(1)} all-gather(f32[1,4,4]{2,1,0:T(4,128)S(1)} %reshape.76), channel_id=1, replica_groups=mesh['grp'=2,'sp_0'=4,'sp_1'=32,'ch'=2] {'sp_1'}, dimensions={0}, use_global_device_ids=true | all-gather | bytes 2112 | tf_op jit(solution)/shard_map/all_gather | solution.py:36
  532.4 0.1 copy.42
  532.5 25.2 %all_gather.15 = f32[256,4]{0,1:T(4,128)S(1)} all-gather(f32[128,4]{0,1:T(4,128)S(1)} %copy.42), channel_id=1, replica_groups=mesh['grp'=2,'sp_0'=4,'sp_1'=32,'ch'=2] {'ch'}, dimensions={0}, use_global_device_ids=true | all-gather | bytes 6144 | tf_op jit(solution)/shard_map/all_gather | solution.py:36
  557.7 0.1 reshape.61
  557.8 0.6 copy.43
  558.4 0.2 reshape_reshape.3
  559.3 0.1 fusion.76
  559.3 0.0 all-to-all-done.1
  559.4 1.1 reshape.85
  560.4 0.3 copy.68
  560.7 1.1 fusion.20
  561.8 1.9 copy.40
  563.7 0.0 copy-start.4
  563.7 4.3 fusion.8
  568.0 0.0 copy-start.3
  568.0 0.1 copy.67
  568.1 4.8 all_to_all.53
  572.9 0.0 copy-done.4
  572.9 0.0 copy-done.3
  572.9 2.2 add_convert_fusion
  (4 shorter events, 0.0 us)
Async XLA Ops:
  6.5 276.4 %all-gather.4.cloned.1.call-start = ((), (), s32[]{:S(2)}) async-start(), calls=%async_computation.3 | async-start | bytes 4227072 | tf_op jit(solution)/shard_map/all_gather | solution.py:24
  287.8 105.0 %copy-start = (bf16[16,64,1,512]{3,1,2,0:T(8,128)(2,1)S(1)}, bf16[16,64,1,512]{3,1,2,0:T(8,128)(2,1)}, u32[]{:S(2)}) copy-start(bf16[16,64,1,512]{3,1,2,0:T(8,128)(2,1)} %param.9) | copy-start | bytes 3145732
  397.9 17.5 %copy-start.1 = (bf16[4,32768]{1,0:T(4,128)(2,1)S(1)}, bf16[4,32768]{1,0:T(4,128)(2,1)}, u32[]{:S(2)}) copy-start(bf16[4,32768]{1,0:T(4,128)(2,1)} %param.13) | copy-start | bytes 786436
  399.1 160.3 %all-to-all-start.1 = ((bf16[128,2,2048]{2,1,0:T(2,128)(2,1)}), bf16[128,2,2048]{2,1,0:T(2,128)(2,1)S(1)}, u32[]{:S(2)}, u32[]{:S(2)}) async-start(bf16[128,2,2048]{2,1,0:T(2,128)(2,1)} %reshape.84), calls=%async_computation.1 | async-start | bytes 2097152 | tf_op jit(solution)/shard_map/all_to_all | solution.py:88
  415.3 7.7 %copy-start.2 = (s32[256]{0:T(256)S(1)}, s32[256]{0:T(256)}, u32[]{:S(2)}) copy-start(s32[256]{0:T(256)} %param.14) | copy-start | bytes 3076
  563.7 9.3 %copy-start.4 = (bf16[1024,1024]{1,0:T(8,128)(2,1)S(1)}, bf16[1024,1024]{1,0:T(8,128)(2,1)}, u32[]{:S(2)}) copy-start(bf16[1024,1024]{1,0:T(8,128)(2,1)} %param.8) | copy-start | bytes 6291460
  568.0 4.9 copy-start.3
Sparse Core Ops, SparseCore 0:
  10.3 272.5 all-gather.3
where the time goes:
time: 583 us; the launch traced here: 582 us
  waiting for transfers between devices  275 us (47%)
  blocking collectives  238 us (41%)
  local copies, waits for them, and re-layouts  19.3 us (3%)
  starting transfers between devices  16.2 us (3%)
  matrix products  15.2 us (3%)
  between operations  14.9 us (3%)
    all_gather x1, waiting for transfers between devices, in_one_piece(): lax.all_gather(both, axis, axis=dim, tiled=True)  275 us
    all_gather x2, blocking collectives, gather_in_order(): parts = lax.all_gather(parts, axes[k], axis=0, tiled=True)  123 us
    all_to_all x1, blocking collectives, local(): lax.all_to_all(width_spec, SP, split_axis=1, concat_axis=0, tiled=True)  104 us
    all_to_all x1, starting transfers between devices, local(): lax.all_to_all(height_back.reshape(TT * HH, band_count, chan_part), SP, s...  16.2 us
  transfers between devices with their start and end apart: 2, of which 1 were waited for; matrix products, arithmetic and copies ran while one was open for 2% of the time, Pallas kernels for 0%

commit v1 on v0

--- a/solution.py
+++ b/solution.py
@@ -13,6 +13,13 @@
 SP_CH = ("sp_0", "sp_1", "ch")
 GRP_SP = ("grp", "sp_0", "sp_1")
 GRP_SP_CH = ("grp", "sp_0", "sp_1", "ch")
+
+
+def gather_over(value, name, dim):
+    devices = lax.axis_size(name)
+    blocks = jnp.stack([value for _ in range(devices)])
+    blocks = lax.all_to_all(blocks, name, split_axis=0, concat_axis=0)
+    return jnp.concatenate(blocks, axis=dim)
 
 
 def in_one_piece(arrays, axis, dim, along):
@@ -33,7 +40,7 @@
 def gather_in_order(value, axes, sequence):
     parts = value[None]
     for k in sequence:
-        parts = lax.all_gather(parts, axes[k], axis=0, tiled=True)
+        parts = gather_over(parts, axes[k], 0)
     held = [lax.axis_size(axes[k]) for k in reversed(sequence)]
     parts = parts.reshape(*held, *value.shape)
     turned = sorted(range(len(sequence)), key=lambda place: sequence[len(sequence) - 1 - place])

time: 583 us -> 569 us (0.976)
  blocking collectives: 238 us -> 14 us
  waiting for transfers between devices: 275 us -> 397 us
  starting transfers between devices: 16.2 us -> 102 us
    all_gather x2 -> x0, blocking collectives: 123 us -> none  [gather_in_order(): parts = lax.all_gather(parts, axes[k], axis=0, tiled=True)]
    all_to_all x1, waiting for transfers between devices: 0.01 us -> 101 us  [local(): lax.all_to_all(height_back.reshape(TT * HH, band_count, chan_part), SP, s...]
    all_to_all x1, blocking collectives: 104 us -> 6.24 us  [gather_over(): blocks = lax.all_to_all(blocks, name, split_axis=0, concat_axis=0)]
    all_to_all x0 -> x3, starting transfers between devices: none -> 89.4 us  [the longest x2 69.9 us: gather_over(): blocks = lax.all_to_all(blocks, name, split_axis=0, concat_axis=0)]
    all_to_all x0 -> x3, waiting for transfers between devices: none -> 84.2 us  [the longest x1 84.2 us: local(): lax.all_to_all(width_spec, SP, split_axis=1, concat_axis=0, tiled=True)]
    all_gather x1, waiting for transfers between devices: 275 us -> 211 us  [in_one_piece(): lax.all_gather(both, axis, axis=dim, tiled=True)]
    unnamed x1 -> x0, blocking collectives: 6.2 us -> none
  transfers between devices with their start and end apart: 2 -> 5, of which waited for: 1 -> 3; matrix products, arithmetic and copies ran while one was open for 2% -> 5% of each run, Pallas kernels for 0% -> 0%
where the time goes in v1:
time: 569 us; the launch traced here: 567 us
  waiting for transfers between devices  397 us (70%)
  starting transfers between devices  102 us (18%)
  local copies, waits for them, and re-layouts  20.4 us (4%)
  matrix products  15.8 us (3%)
  between operations  14.2 us (2%)
  blocking collectives  14 us (2%)
    all_gather x1, waiting for transfers between devices, in_one_piece(): lax.all_gather(both, axis, axis=dim, tiled=True)  211 us
    all_to_all x1, waiting for transfers between devices, local(): lax.all_to_all(height_back.reshape(TT * HH, band_count, chan_part), SP, s...  101 us
    all_to_all x1, waiting for transfers between devices, local(): lax.all_to_all(width_spec, SP, split_axis=1, concat_axis=0, tiled=True)  84.2 us
    all_to_all x2, starting transfers between devices, gather_over(): blocks = lax.all_to_all(blocks, name, split_axis=0, concat_axis=0)  69.9 us
    all_to_all x1, starting transfers between devices, local(): lax.all_to_all(width_spec, SP, split_axis=1, concat_axis=0, tiled=True)  19.6 us
    all_to_all x1, starting transfers between devices, local(): lax.all_to_all(height_back.reshape(TT * HH, band_count, chan_part), SP, s...  12.4 us
  transfers between devices with their start and end apart: 5, of which 3 were waited for; matrix products, arithmetic and copies ran while one was open for 5% of the time, Pallas kernels for 0%

profile of v1, /device:TPU:39, one launch (start us, length us, event | category | flops | bytes accessed | tf_op | source)
XLA Modules:
  0.0 566.6 jit_solution(611881971577746218)
XLA Ops:
  6.5 0.0 all-gather.2.cloned.1.call-start
  6.6 1.3 pad_maximum_fusion
  7.9 0.1 all-gather.2.cloned.1.call-update
  8.0 0.0 copy-start
  8.0 0.0 copy-start.2
  8.0 6.7 %copy.52 = bf16[4,32768]{0,1:T(8,128)(2,1)} copy(bf16[4,32768]{1,0:T(4,128)(2,1)} %param.13) | data formatting | bytes 524288 | tf_op args[5]
  14.7 0.0 copy-done
  14.7 5.2 gather_fusion
  19.9 0.1 convert_reduce_fusion
  20.0 6.2 %all_to_all.67 = f32[4,1,4]{2,1,0:T(1,128)S(1)} all-to-all(f32[4,1,4]{2,1,0:T(1,128)S(1)} %stack.9), channel_id=1, replica_groups=mesh['grp'=2,'sp_0'=4,'sp_1'=32,'ch'=2] {'sp_0'}, dimensions={0} | all-to-all | bytes 128 | tf_op jit(solution)/shard_map/all_to_all | solution.py:21
  26.3 0.1 copy.53
  26.4 0.6 stack.10
  27.0 45.5 %all-to-all-start.3 = ((f32[32,4,4]{1,2,0:T(4,128)}), f32[32,4,4]{1,2,0:T(4,128)S(1)}, u32[]{:S(2)}, u32[]{:S(2)}) async-start(f32[32,4,4]{1,2,0:T(4,128)} %stack.10), calls=%async_computation.3 | async-start | bytes 131072 | tf_op jit(solution)/shard_map/all_to_all | solution.py:21
  72.5 211.1 %all-gather.2.cloned.1.call-done = bf16[1024,2048]{1,0:T(8,128)(2,1)} async-done(((bf16[8,2048]{1,0:T(8,128)(2,1)}), bf16[1024,2048]{1,0:T(8,128)(2,1)}) %all-gather.2.cloned.1.call-update) | async-done | bytes 4194320 | tf_op jit(solution)/shard_map/all_gather | solution.py:31
  283.6 0.0 copy-done.2
  283.6 2.5 fusion.11
  286.2 0.7 fusion.12
  286.9 1.7 copy.45
  288.6 0.0 all-to-all-done.3
  288.6 19.6 %all-to-all-start = ((bf16[8,128,512]{2,0,1:T(8,128)(2,1)}), bf16[8,128,512]{2,0,1:T(8,128)(2,1)S(1)}, u32[]{:S(2)}, u32[]{:S(2)}) async-start(bf16[8,128,512]{2,0,1:T(8,128)(2,1)} %copy.45), calls=%async_computation | async-start | bytes 2097152 | tf_op jit(solution)/shard_map/all_to_all | solution.py:87
  308.2 0.1 stack_reshape.5
  308.3 0.6 pad_maximum_fusion.1
  308.9 84.2 %all-to-all-done = bf16[8,128,512]{2,0,1:T(8,128)(2,1)S(1)} async-done(((bf16[8,128,512]{2,0,1:T(8,128)(2,1)}), bf16[8,128,512]{2,0,1:T(8,128)(2,1)S(1)}, u32[]{:S(2)}, u32[]{:S(2)}) %all-to-all-start) | async-done | bytes 1048608 | tf_op jit(solution)/shard_map/all_to_all | solution.py:87
  393.0 24.4 %all-to-all-start.4 = ((f32[2,128,4]{1,2,0:T(4,128)}), f32[2,128,4]{1,2,0:T(4,128)S(1)}, u32[]{:S(2)}, u32[]{:S(2)}) async-start(f32[2,128,4]{1,2,0:T(4,128)} %pad_maximum_fusion.1), calls=%async_computation.4 | async-start | bytes 8192 | tf_op jit(solution)/shard_map/all_to_all | solution.py:21
  417.4 0.5 fusion.14
  418.0 2.8 convolution_convert_fusion.2
  420.8 1.5 convolution_convert_fusion
  422.3 0.5 broadcast.88
  422.8 1.5 reduce.1
  424.3 1.2 reshape.70
  425.5 0.0 all-to-all-done.4
  425.5 12.4 %all-to-all-start.1 = ((bf16[128,2,2048]{2,1,0:T(2,128)(2,1)}), bf16[128,2,2048]{2,1,0:T(2,128)(2,1)S(1)}, u32[]{:S(2)}, u32[]{:S(2)}) async-start(bf16[128,2,2048]{2,1,0:T(2,128)(2,1)} %reshape.70), calls=%async_computation.1 | async-start | bytes 2097152 | tf_op jit(solution)/shard_map/all_to_all | solution.py:95
  438.5 0.1 reshape_reshape.6
  438.7 0.6 copy.55
  439.3 0.2 reshape_reshape.7
  439.5 0.1 fusion.76
  439.5 101.5 %all-to-all-done.1 = bf16[128,2,2048]{2,1,0:T(2,128)(2,1)S(1)} async-done(((bf16[128,2,2048]{2,1,0:T(2,128)(2,1)}), bf16[128,2,2048]{2,1,0:T(2,128)(2,1)S(1)}, u32[]{:S(2)}, u32[]{:S(2)}) %all-to-all-start.1) | async-done | bytes 1048608 | tf_op jit(solution)/shard_map/all_to_all | solution.py:95
  541.0 1.0 reshape.71
  542.1 0.3 copy.80
  542.4 1.1 fusion.20
  543.5 1.9 copy.51
  545.3 4.3 fusion.8
  549.7 0.0 copy-start.1
  549.7 0.1 copy.79
  549.7 7.7 %all_to_all.68 = bf16[2,512,512]{1,2,0:T(8,128)(2,1)S(1)} all-to-all(bf16[2,512,512]{1,2,0:T(8,128)(2,1)S(1)} %bitcast.99), channel_id=1, replica_groups=mesh['grp'=2,'sp_0'=4,'sp_1'=32,'ch'=2] {'ch'}, dimensions={0} | all-to-all | bytes 2097152 | tf_op jit(solution)/shard_map/all_to_all | solution.py:111
  557.5 0.0 copy-done.3
  557.5 0.0 copy-done.1
  557.5 2.3 add_convert_fusion
  (7 shorter events, 0.0 us)
Async XLA Ops:
  6.5 277.1 %all-gather.2.cloned.1.call-start = ((), (), s32[]{:S(2)}) async-start(), calls=%async_computation.6 | async-start | bytes 4227072 | tf_op jit(solution)/shard_map/all_gather | solution.py:31
  8.0 6.7 %copy-start = (s32[256]{0:T(256)S(1)}, s32[256]{0:T(256)}, u32[]{:S(2)}) copy-start(s32[256]{0:T(256)} %param.14) | copy-start | bytes 3076
  8.0 275.6 %copy-start.2 = (bf16[1024,1024]{1,0:T(8,128)(2,1)S(1)}, bf16[1024,1024]{1,0:T(8,128)(2,1)}, u32[]{:S(2)}) copy-start(bf16[1024,1024]{1,0:T(8,128)(2,1)} %param.8) | copy-start | bytes 6291460
  27.0 261.5 %all-to-all-start.3 = ((f32[32,4,4]{1,2,0:T(4,128)}), f32[32,4,4]{1,2,0:T(4,128)S(1)}, u32[]{:S(2)}, u32[]{:S(2)}) async-start(f32[32,4,4]{1,2,0:T(4,128)} %stack.10), calls=%async_computation.3 | async-start | bytes 131072 | tf_op jit(solution)/shard_map/all_to_all | solution.py:21
  288.6 104.5 %all-to-all-start = ((bf16[8,128,512]{2,0,1:T(8,128)(2,1)}), bf16[8,128,512]{2,0,1:T(8,128)(2,1)S(1)}, u32[]{:S(2)}, u32[]{:S(2)}) async-start(bf16[8,128,512]{2,0,1:T(8,128)(2,1)} %copy.45), calls=%async_computation | async-start | bytes 2097152 | tf_op jit(solution)/shard_map/all_to_all | solution.py:87
  393.0 32.5 %all-to-all-start.4 = ((f32[2,128,4]{1,2,0:T(4,128)}), f32[2,128,4]{1,2,0:T(4,128)S(1)}, u32[]{:S(2)}, u32[]{:S(2)}) async-start(f32[2,128,4]{1,2,0:T(4,128)} %pad_maximum_fusion.1), calls=%async_computation.4 | async-start | bytes 8192 | tf_op jit(solution)/shard_map/all_to_all | solution.py:21
  425.5 115.5 %all-to-all-start.1 = ((bf16[128,2,2048]{2,1,0:T(2,128)(2,1)}), bf16[128,2,2048]{2,1,0:T(2,128)(2,1)S(1)}, u32[]{:S(2)}, u32[]{:S(2)}) async-start(bf16[128,2,2048]{2,1,0:T(2,128)(2,1)} %reshape.70), calls=%async_computation.1 | async-start | bytes 2097152 | tf_op jit(solution)/shard_map/all_to_all | solution.py:95
  545.3 12.2 %copy-start.3 = (bf16[1024,1024]{1,0:T(8,128)(2,1)S(1)}, bf16[1024,1024]{1,0:T(8,128)(2,1)}, u32[]{:S(2)}) copy-start(bf16[1024,1024]{1,0:T(8,128)(2,1)} %param.8) | copy-start | bytes 6291460
  549.7 7.8 %copy-start.1 = (bf16[1024,2048]{1,0:T(8,128)(2,1)S(1)}, bf16[1024,2048]{1,0:T(8,128)(2,1)}, u32[]{:S(2)}) copy-start(bf16[1024,2048]{1,0:T(8,128)(2,1)} %all-gather.2.cloned.1.call-done) | copy-start | bytes 12582916
Sparse Core Ops, SparseCore 0:
  10.3 273.2 all-gather.1
